TPU v7x, 256 devices: a whole 4x4x8 slice. The times are simulated.
256 devices in a mesh: cfg: 2 (over y_hi), seq: 16 (over z, core), tp: 8 (over y_lo, x).
Axes of the slice: x: 4, y: 4 (y_hi: 2, y_lo: 2; y = y_hi * 2 + y_lo), z: 8, core: 2. Of those that a mesh axis runs over, the one named last changes fastest.
Arguments:
- queries: bfloat16 [2, 7680, 5120], P('cfg', 'seq', 'tp'), may hold values from -5 to 5
- keys: bfloat16 [2, 7680, 5120], P('cfg', 'seq', 'tp'), may hold values from -5 to 5
- values: bfloat16 [2, 7680, 5120], P('cfg', 'seq', 'tp'), may hold values from -5 to 5
- text_keys: bfloat16 [2, 512, 5120], P('cfg', None, 'tp'), may hold values from -7.5 to 7.5
- text_values: bfloat16 [2, 512, 5120], P('cfg', None, 'tp'), may hold values from -5 to 5
- prompt_lengths: int32 [2], P('cfg'), may hold values from 64 to 512
- frame_counts: int32 [16], P('seq'), may hold values from 240 to 480
- out_weight: bfloat16 [5120, 5120], P('tp'), may hold values from -0.5 to 0.5
Outputs:
- velocity: bfloat16 [7680, 5120], P('seq', ('tp', 'cfg'))
All inputs are finite; a program needn't handle non-finite values.
Results may differ from a plain program's by a relative error of at most 0.015.
Values may be sent and summed in bfloat16 or wider, within the bound.
A program may use at most 256 MiB of HBM per device.

v0:
```python
import jax
import jax.numpy as jnp
from jax import lax
from jax.sharding import PartitionSpec as P

HEAD_DIM = 128
FRAME_SLOTS = 480
GUIDANCE = 5.0
RESCALE = 0.7
NEGATIVE = -1e30


def in_order(pieces, dim):
    dims = list(pieces.shape[1:])
    dims[dim] *= pieces.shape[0]
    return jnp.moveaxis(pieces, 0, dim).reshape(dims)


def from_everyone(value, axis):
    devices = lax.axis_size(axis)
    return lax.all_to_all(
        jnp.broadcast_to(value[None], (devices, *value.shape)), axis, 0, 0, tiled=True
    )


def gathered_copies(value, axis, dim):
    return in_order(from_everyone(value, axis), dim)


def of_everyone(value, axis):
    return from_everyone(value, axis).sum(axis=0)


def together(arrays, axis):
    ends = [0]
    for a in arrays:
        ends.append(ends[-1] + a.size)
    running = of_everyone(jnp.concatenate([a.ravel() for a in arrays]), axis)
    return tuple((running[b:e].reshape(a.shape) for a, b, e in zip(arrays, ends, ends[1:])))


def frame_valid(positions, counts_table):
    frame_index = positions // FRAME_SLOTS
    slot_index = positions % FRAME_SLOTS
    frame_ids = jnp.arange(counts_table.shape[0], dtype=jnp.int32)
    frame_limit = jnp.sum(
        jnp.where(frame_index[:, None] == frame_ids[None, :], counts_table[None, :], 0), axis=1
    )
    return slot_index < frame_limit


def attend_block(carry, key_rows, value_rows, query_heads, key_mask):
    row_max, weight_sum, mixed_sum = carry
    head_count = query_heads.shape[1]
    key_heads = key_rows.reshape(key_rows.shape[0], head_count, HEAD_DIM)
    value_heads = value_rows.reshape(value_rows.shape[0], head_count, HEAD_DIM)
    scores = jnp.einsum(
        "qhd,khd->hqk", query_heads, key_heads, preferred_element_type=jnp.float32
    ) * HEAD_DIM ** (-0.5)
    scores = jnp.where(key_mask[None, None, :], scores, NEGATIVE)
    new_max = jnp.maximum(row_max, jnp.max(scores, axis=2))
    shrink = jnp.exp(row_max - new_max)
    weights = jnp.exp(scores - new_max[:, :, None])
    weight_sum = weight_sum * shrink + jnp.sum(weights, axis=2)
    mixed_sum = mixed_sum * shrink[:, :, None] + jnp.einsum(
        "hqk,khd->hqd",
        weights.astype(jnp.bfloat16),
        value_heads,
        preferred_element_type=jnp.float32,
    )
    return (new_max, weight_sum, mixed_sum)


def body(queries, keys, values, text_keys, text_values, prompt_lengths, frame_counts, out_weight):
    row_count = queries.shape[1]
    head_cols = queries.shape[2]
    head_count = head_cols // HEAD_DIM
    all_counts = gathered_copies(frame_counts, "seq", 0)
    query_heads = queries[0].reshape(row_count, head_count, HEAD_DIM)
    text_mask = jnp.arange(text_keys.shape[1], dtype=jnp.int32) < prompt_lengths[0]
    empty_state = (
        jnp.full((head_count, row_count), NEGATIVE, jnp.float32),
        jnp.zeros((head_count, row_count), jnp.float32),
        jnp.zeros((head_count, row_count, HEAD_DIM), jnp.float32),
    )
    text_state = attend_block(empty_state, text_keys[0], text_values[0], query_heads, text_mask)
    key_rows = lax.all_gather(keys[0], "seq", axis=0, tiled=True)
    value_rows = lax.all_gather(values[0], "seq", axis=0, tiled=True)
    positions = jnp.arange(key_rows.shape[0], dtype=jnp.int32)
    row_max, weight_sum, mixed_sum = attend_block(
        text_state, key_rows, value_rows, query_heads, frame_valid(positions, all_counts)
    )
    attended = (
        jnp.transpose(mixed_sum / weight_sum[:, :, None], (1, 0, 2))
        .reshape(row_count, head_cols)
        .astype(jnp.bfloat16)
    )
    projected = (
        lax.psum_scatter(
            lax.dot_general(
                out_weight, attended, (((0,), (1,)), ((), ())), preferred_element_type=jnp.float32
            ).astype(jnp.bfloat16),
            "tp",
            scatter_dimension=0,
            tiled=True,
        )
        .astype(jnp.float32)
        .T
    )
    branch = projected.astype(jnp.bfloat16)[None]
    paired = lax.all_to_all(branch, "cfg", split_axis=2, concat_axis=0, tiled=True)
    conditional = paired[0].astype(jnp.float32)
    unconditional = paired[1].astype(jnp.float32)
    guided = unconditional + GUIDANCE * (conditional - unconditional)
    token_weights = frame_valid(jnp.arange(row_count, dtype=jnp.int32), frame_counts).astype(
        jnp.float32
    )

    def local_sum(field_rows):
        return jnp.dot(token_weights, field_rows)

    guided_sum, guided_square, cond_sum, cond_square = together(
        (
            local_sum(guided),
            local_sum(guided * guided),
            local_sum(conditional),
            local_sum(conditional * conditional),
        ),
        "seq",
    )
    valid_total = jnp.sum(all_counts).astype(jnp.float32)
    guided_mean = guided_sum / valid_total
    guided_var = guided_square / valid_total - guided_mean * guided_mean
    cond_mean = cond_sum / valid_total
    cond_var = cond_square / valid_total - cond_mean * cond_mean
    std_ratio = jnp.sqrt((cond_var + 1.0) / (guided_var + 1.0))
    factor = RESCALE * std_ratio + (1.0 - RESCALE)
    return (guided_mean + (guided - guided_mean) * factor).astype(jnp.bfloat16)


def solution(mesh):
    placed = (
        P("cfg", "seq", "tp"),
        P("cfg", "seq", "tp"),
        P("cfg", "seq", "tp"),
        P("cfg", None, "tp"),
        P("cfg", None, "tp"),
        P("cfg"),
        P("seq"),
        P("tp", None),
    )
    return jax.shard_map(
        body, mesh=mesh, in_specs=placed, out_specs=P("seq", ("tp", "cfg")), check_vma=False
    )
```

profile of v0, /device:TPU:1, one launch (start us, length us, event | category | flops | bytes accessed | tf_op | source)
XLA Modules:
  0.0 327.0 jit_solution(5678599585954011462)
XLA Ops:
  9.3 10.0 %all-to-all-start = ((s32[16,1,1]{2,1,0:T(1,128)}), s32[16,1,1]{2,1,0:T(1,128)S(1)}, u32[]{:S(2)}, u32[]{:S(2)}) async-start(s32[16,1,1]{2,1,0:T(1,128)} %broadcast_in_dim.95), calls=%async_computation | async-start | bytes 16384 | tf_op jit(solution)/shard_map/all_to_all | solution.py:21
  19.3 1.3 copy.70
  21.2 1.3 copy.71
  22.6 3.2 fusion.7
  27.4 48.6 %all-gather.5.cloned.1.call-done = bf16[1,7680,640]{2,1,0:T(8,128)(2,1)} async-done(((bf16[1,480,640]{2,1,0:T(8,128)(2,1)}), bf16[1,7680,640]{2,1,0:T(8,128)(2,1)}) %all-gather.5.cloned.1.call-update) | async-done | bytes 9830416 | tf_op jit(solution)/shard_map/all_gather | solution.py:87
  76.0 13.7 %copy.76 = bf16[1,7680,640]{1,2,0:T(8,128)(2,1)} copy(bf16[1,7680,640]{2,1,0:T(8,128)(2,1)} %all-gather.5.cloned.1.call-done) | data formatting | bytes 19660800 | tf_op jit(solution)/shard_map/all_gather | solution.py:87
  89.8 31.7 %fusion = (f32[5,480]{1,0:T(8,128)S(1)}, f32[5,480,7680]{2,1,0:T(8,128)}) fusion(pred[7680]{0:T(1024)(128)(4,1)S(1)} %fusion.41, bf16[480,5,128]{0,2,1:T(8,128)(2,1)S(1)} %bitcast.102, bf16[7680,5,128]{0,2,1:T(8,128)(2,1)} %bitcast.97), kind=kOutput, calls=%fused_computation.2 | convolution fusion | flops 4773885440 | bytes 84190080 | tf_op jit(solution)/shard_map/qhd,khd->hqk/dot_general | solution.py:57
  121.5 3.9 %fusion.8 = f32[5,480]{1,0:T(8,128)S(1)} fusion(f32[5,480,512]{2,1,0:T(8,128)} %get-tuple-element.17, f32[5,480]{1,0:T(8,128)S(1)} %get-tuple-element.11, pred[512]{0:T(512)(128)(4,1)S(1)} %iota_compare_fusion.2), kind=kLoop, calls=%fused_computation.12 | loop fusion | flops 4912800 | bytes 4934912 | tf_op jit(solution)/shard_map/reduce_sum | solution.py:64
  125.4 23.8 %fusion.1 = f32[5,480]{1,0:T(8,128)S(1)} fusion(f32[5,480,7680]{2,1,0:T(8,128)} %get-tuple-element.15, f32[5,480]{1,0:T(8,128)S(1)} %get-tuple-element.10, pred[7680]{0:T(1024)(128)(4,1)S(1)} %fusion.41), kind=kLoop, calls=%fused_computation.3 | loop fusion | flops 73725600 | bytes 73754880 | tf_op jit(solution)/shard_map/reduce_sum | solution.py:64
  149.3 1.7 fusion.28
  151.0 13.7 %copy.79 = bf16[1,7680,640]{1,2,0:T(8,128)(2,1)} copy(bf16[1,7680,640]{2,1,0:T(8,128)(2,1)} %all-gather.7.cloned.1.call-done) | data formatting | bytes 19660800 | tf_op jit(solution)/shard_map/all_gather | solution.py:88
  164.7 29.4 %fusion.34 = bf16[480,5,128]{2,0,1:T(8,128)(2,1)S(1)} fusion(f32[480,5,128]{2,0,1:T(8,128)S(1)} %fusion.28, bf16[7680,5,128]{0,2,1:T(8,128)(2,1)} %bitcast.100, f32[5,480,7680]{2,1,0:T(8,128)} %get-tuple-element.15, f32[5,480]{1,0:T(8,128)S(1)} %get-tuple-element.10, pred[7680]{0:T(1024)(128)(4,1)S(1)} %fusion.41, f32[480,5]{0,1:T(8,128)S(1)} %get-tuple-element.7), kind=kOutput, calls=%fused_computation.25 | convolution fusion | flops 4793241600 | bytes 85428480 | tf_op jit(solution)/shard_map/hqk,khd->hqd/dot_general | solution.py:65
  194.3 8.8 %fusion.6 = bf16[5120,480]{0,1:T(8,128)(2,1)} fusion(bf16[480,640]{0,1:T(8,128)(2,1)S(1)} %bitcast.116, bf16[640,5120]{1,0:T(8,128)(2,1)} %param.15), kind=kOutput, calls=%fused_computation.8 | convolution fusion | flops 3148185600 | bytes 12083200 | tf_op jit(solution)/shard_map/dot_general | solution.py:100
  203.2 7.8 %copy.91 = bf16[5120,480]{1,0:T(8,128)(2,1)} copy(bf16[5120,480]{0,1:T(8,128)(2,1)} %fusion.6) | data formatting | bytes 9830400
  211.0 64.1 %reduce-scatter.4.cloned.1.call-done = bf16[640,480]{1,0:T(8,128)(2,1)} async-done(((bf16[5120,480]{1,0:T(8,128)(2,1)}), bf16[640,480]{1,0:T(8,128)(2,1)}) %reduce-scatter.4.cloned.1.call-update) | async-done | bytes 614416
  275.1 1.4 copy.92
  276.5 1.9 copy.82
  278.9 4.8 %reduce.13 = bf16[640,480]{1,0:T(8,128)(2,1)S(1)} reduce(bf16[640,1,480]{2,1,0:T(2,128)(2,1)S(1)} %bitcast.103, bf16[]{:T(256)} %broadcast.122), dimensions={1}, to_apply=%bitcast.78.reduce_sub_computation | reduce | bytes 1228802
  283.7 2.2 reshape.116
  285.9 3.7 %all-to-all-start.1 = ((bf16[2,2,76800]{2,1,0:T(2,128)(2,1)}), bf16[2,2,76800]{2,1,0:T(2,128)(2,1)S(1)}, u32[]{:S(2)}, u32[]{:S(2)}) async-start(bf16[2,2,76800]{2,1,0:T(2,128)(2,1)} %reshape.116), calls=%async_computation.1 | async-start | bytes 1228800 | tf_op jit(solution)/shard_map/all_to_all | solution.py:111
  289.7 9.5 %all-to-all-done.1 = bf16[2,2,76800]{2,1,0:T(2,128)(2,1)S(1)} async-done(((bf16[2,2,76800]{2,1,0:T(2,128)(2,1)}), bf16[2,2,76800]{2,1,0:T(2,128)(2,1)S(1)}, u32[]{:S(2)}, u32[]{:S(2)}) %all-to-all-start.1) | async-done | bytes 614432 | tf_op jit(solution)/shard_map/all_to_all | solution.py:111
  299.2 1.3 reshape.117
  302.4 8.9 %all-to-all-start.2 = ((f32[16,1,1280]{2,1,0:T(1,128)}), f32[16,1,1280]{2,1,0:T(1,128)S(1)}, u32[]{:S(2)}, u32[]{:S(2)}) async-start(f32[16,1,1280]{2,1,0:T(1,128)} %broadcast_in_dim.102), calls=%async_computation.2 | async-start | bytes 163840 | tf_op jit(solution)/shard_map/all_to_all | solution.py:21
  311.9 7.5 %all-to-all-done.2 = f32[16,1,1280]{2,1,0:T(1,128)S(1)} async-done(((f32[16,1,1280]{2,1,0:T(1,128)}), f32[16,1,1280]{2,1,0:T(1,128)S(1)}, u32[]{:S(2)}, u32[]{:S(2)}) %all-to-all-start.2) | async-done | bytes 81952 | tf_op jit(solution)/shard_map/all_to_all | solution.py:21
  (38 shorter events, 7.4 us)
Async XLA Ops:
  6.5 19.3 %copy-start = (bf16[1,512,640]{2,1,0:T(8,128)(2,1)S(1)}, bf16[1,512,640]{2,1,0:T(8,128)(2,1)}, u32[]{:S(2)}) copy-start(bf16[1,512,640]{2,1,0:T(8,128)(2,1)} %param.12) | copy-start | bytes 1966084
  6.5 69.5 %all-gather.5.cloned.1.call-start = ((), (), s32[]{:S(2)}) async-start(), calls=%async_computation.4 | async-start | bytes 10444800 | tf_op jit(solution)/shard_map/all_gather | solution.py:87
  7.3 143.7 %all-gather.7.cloned.1.call-start = ((), (), s32[]{:S(2)}) async-start(), calls=%async_computation.5 | async-start | bytes 10444800 | tf_op jit(solution)/shard_map/all_gather | solution.py:88
  9.3 16.9 %all-to-all-start = ((s32[16,1,1]{2,1,0:T(1,128)}), s32[16,1,1]{2,1,0:T(1,128)S(1)}, u32[]{:S(2)}, u32[]{:S(2)}) async-start(s32[16,1,1]{2,1,0:T(1,128)} %broadcast_in_dim.95), calls=%async_computation | async-start | bytes 16384 | tf_op jit(solution)/shard_map/all_to_all | solution.py:21
  19.2 255.8 %reduce-scatter.4.cloned.1.call-start = ((), (), s32[]{:S(2)}) async-start(), calls=%async_computation.6 | async-start | bytes 5898240
  121.5 27.8 %slice-start = ((s8[4915200]{0:T(1024)(128)(4,1)}), s8[4194304]{0:T(1024)(128)(4,1)S(1)}, s32[]{:S(2)}) async-start(s8[4915200]{0:T(1024)(128)(4,1)} %bitcast.98), calls=%async_computation.7 | async-start | bytes 8388608
  125.4 23.9 %slice-start.1 = ((s8[4915200]{0:T(1024)(128)(4,1)}), s8[720896]{0:T(1024)(128)(4,1)S(1)}, s32[]{:S(2)}) async-start(s8[4915200]{0:T(1024)(128)(4,1)} %bitcast.98), calls=%async_computation.8 | async-start | bytes 1441792
  285.9 13.3 %all-to-all-start.1 = ((bf16[2,2,76800]{2,1,0:T(2,128)(2,1)}), bf16[2,2,76800]{2,1,0:T(2,128)(2,1)S(1)}, u32[]{:S(2)}, u32[]{:S(2)}) async-start(bf16[2,2,76800]{2,1,0:T(2,128)(2,1)} %reshape.116), calls=%async_computation.1 | async-start | bytes 1228800 | tf_op jit(solution)/shard_map/all_to_all | solution.py:111
  302.4 17.0 %all-to-all-start.2 = ((f32[16,1,1280]{2,1,0:T(1,128)}), f32[16,1,1280]{2,1,0:T(1,128)S(1)}, u32[]{:S(2)}, u32[]{:S(2)}) async-start(f32[16,1,1280]{2,1,0:T(1,128)} %broadcast_in_dim.102), calls=%async_computation.2 | async-start | bytes 163840 | tf_op jit(solution)/shard_map/all_to_all | solution.py:21
Sparse Core Ops, SparseCore 0:
  9.2 66.8 all-gather.4
  77.9 61.1 all-gather.6
  211.1 63.8 reduce-scatter.3
where the time goes:
time: 328 us; the launch traced here: 327 us
  waiting for transfers between devices  131 us (40%)
  matrix products  75.7 us (23%)
  local copies, waits for them, and re-layouts  47.3 us (14%)
  other arithmetic  34.9 us (11%)
  starting transfers between devices  22.6 us (7%)
  between operations  15.2 us (5%)
    unnamed x4, waiting for transfers between devices  65.5 us
    all_gather x1, waiting for transfers between devices, body(): key_rows = lax.all_gather(keys[0], 'seq', axis=0, tiled=True)  48.6 us
    dot_general x2, matrix products, attend_block(): jnp.einsum('qhd,khd->hqk', query_heads, key_heads, preferred_element_type...  34.9 us
    dot_general x2, matrix products, attend_block(): jnp.einsum('hqk,khd->hqd', weights.astype(jnp.bfloat16), value_heads, pre...  31 us
    reduce_sum x2, other arithmetic, attend_block(): weight_sum = weight_sum * shrink + jnp.sum(weights, axis=2)  27.8 us
    all_to_all x2, starting transfers between devices, from_everyone(): lax.all_to_all(jnp.broadcast_to(value[None], (devices, *value.shape)), ax...  18.8 us
    unnamed x15, local copies, waits for them, and re-layouts  16.3 us
    all_gather x1, local copies, waits for them, and re-layouts, body(): value_rows = lax.all_gather(values[0], 'seq', axis=0, tiled=True)  13.7 us
  transfers between devices with their start and end apart: 6, of which 5 were waited for; matrix products, arithmetic and copies ran while one was open for 25% of the time, Pallas kernels for 0%

commit v1 on v0

--- a/solution.py
+++ b/solution.py
@@ -2,6 +2,7 @@
 import jax.numpy as jnp
 from jax import lax
 from jax.sharding import PartitionSpec as P
+from jax.lax import all_to_all, axis_size
 
 HEAD_DIM = 128
 FRAME_SLOTS = 480
@@ -84,7 +85,9 @@
         jnp.zeros((head_count, row_count, HEAD_DIM), jnp.float32),
     )
     text_state = attend_block(empty_state, text_keys[0], text_values[0], query_heads, text_mask)
-    key_rows = lax.all_gather(keys[0], "seq", axis=0, tiled=True)
+    key_rows = jnp.concatenate(
+        all_to_all(jnp.stack(axis_size("seq") * [keys[0]]), "seq", 0, 0), axis=0
+    )
     value_rows = lax.all_gather(values[0], "seq", axis=0, tiled=True)
     positions = jnp.arange(key_rows.shape[0], dtype=jnp.int32)
     row_max, weight_sum, mixed_sum = attend_block(

time: 328 us -> 557 us (1.70)
  waiting for transfers between devices: 131 us -> 337 us
  blocking collectives: 0 us -> 16.8 us
  local copies, waits for them, and re-layouts: 47.3 us -> 58.5 us
    all_to_all x0 -> x1, waiting for transfers between devices: none -> 254 us  [body(): all_to_all(jnp.stack(axis_size('seq') * [keys[0]]), 'seq', 0, 0)]
    all_gather x1 -> x0, waiting for transfers between devices: 48.6 us -> none  [body(): key_rows = lax.all_gather(keys[0], 'seq', axis=0, tiled=True)]
    another operation x0 -> x2, local copies, waits for them, and re-layouts: none -> 27.6 us  [the longest x1 22 us: attend_block(): key_heads = key_rows.reshape(key_rows.shape[0], head_count, HEAD_DIM)]
    all_to_all x0 -> x1, blocking collectives: none -> 16.8 us  [from_everyone(): lax.all_to_all(jnp.broadcast_to(value[None], (devices, *value.shape)), ax...]
    all_gather x1 -> x0, local copies, waits for them, and re-layouts: 13.7 us -> none  [body(): key_rows = lax.all_gather(keys[0], 'seq', axis=0, tiled=True)]
    all_to_all x2 -> x1, starting transfers between devices: 18.8 us -> 8.92 us  [from_everyone(): lax.all_to_all(jnp.broadcast_to(value[None], (devices, *value.shape)), ax...]
    unnamed x15 -> x19, local copies, waits for them, and re-layouts: 16.3 us -> 14.2 us
    unnamed x4 -> x3, waiting for transfers between devices: 65.5 us -> 65.7 us
  transfers between devices with their start and end apart: 6 -> 5, of which waited for: 5 -> 4; matrix products, arithmetic and copies ran while one was open for 25% -> 16% of each run, Pallas kernels for 0% -> 0%
where the time goes in v1:
time: 557 us; the launch traced here: 556 us
  waiting for transfers between devices  337 us (61%)
  matrix products  76.1 us (14%)
  local copies, waits for them, and re-layouts  58.5 us (11%)
  other arithmetic  34.2 us (6%)
  starting transfers between devices  18 us (3%)
  blocking collectives  16.8 us (3%)
  between operations  15.5 us (3%)
    all_to_all x1, waiting for transfers between devices, body(): all_to_all(jnp.stack(axis_size('seq') * [keys[0]]), 'seq', 0, 0)  254 us
    unnamed x3, waiting for transfers between devices  65.7 us
    dot_general x2, matrix products, attend_block(): jnp.einsum('qhd,khd->hqk', query_heads, key_heads, preferred_element_type...  35.4 us
    dot_general x2, matrix products, attend_block(): jnp.einsum('hqk,khd->hqd', weights.astype(jnp.bfloat16), value_heads, pre...  31 us
    reduce_sum x2, other arithmetic, attend_block(): weight_sum = weight_sum * shrink + jnp.sum(weights, axis=2)  27 us
    another operation x1, local copies, waits for them, and re-layouts, attend_block(): key_heads = key_rows.reshape(key_rows.shape[0], head_count, HEAD_DIM)  22 us
    all_to_all x1, blocking collectives, from_everyone(): lax.all_to_all(jnp.broadcast_to(value[None], (devices, *value.shape)), ax...  16.8 us
    unnamed x19, local copies, waits for them, and re-layouts  14.2 us
  transfers between devices with their start and end apart: 5, of which 4 were waited for; matrix products, arithmetic and copies ran while one was open for 16% of the time, Pallas kernels for 0%

profile of v1, /device:TPU:1, one launch (start us, length us, event | category | flops | bytes accessed | tf_op | source)
XLA Modules:
  0.0 555.7 jit_solution(11802831380905195080)
XLA Ops:
  7.2 16.8 %all_to_all.32 = s32[16,1,1]{2,1,0:T(1,128)S(1)} all-to-all(s32[16,1,1]{2,1,0:T(1,128)S(1)} %broadcast_in_dim.95), channel_id=1, replica_groups=mesh['cfg'=2,'seq'=16,'tp'=8] {'seq'}, dimensions={0} | all-to-all | bytes 128 | tf_op jit(solution)/shard_map/all_to_all | solution.py:22
  24.0 5.6 %stack.3 = bf16[16,480,640]{2,1,0:T(8,128)(2,1)} broadcast(bf16[480,640]{1,0:T(8,128)(2,1)} %bitcast.115), dimensions={1,2} | broadcast | bytes 10444800 | tf_op jit(solution)/shard_map/stack | solution.py:89
  29.6 5.3 all-to-all-start.1
  37.2 3.1 fusion.9
  41.5 253.9 %all-to-all-done.1 = bf16[16,480,640]{2,1,0:T(8,128)(2,1)} async-done(((bf16[16,480,640]{2,1,0:T(8,128)(2,1)}), bf16[16,480,640]{2,1,0:T(8,128)(2,1)}, u32[]{:S(2)}, u32[]{:S(2)}) %all-to-all-start.1) | async-done | bytes 9830432 | tf_op jit(solution)/shard_map/all_to_all | solution.py:89
  295.3 22.0 %reshape.104 = bf16[7680,5,128]{2,1,0:T(8,128)(2,1)} reshape(bf16[16,480,640]{2,1,0:T(8,128)(2,1)} %all-to-all-done.1) | data formatting | bytes 19660800 | tf_op jit(solution)/shard_map/reshape;reshape | solution.py:56
  317.3 32.2 %fusion = (f32[5,480]{1,0:T(8,128)S(1)}, f32[5,480,7680]{2,1,0:T(8,128)}) fusion(pred[7680]{0:T(1024)(128)(4,1)S(1)} %fusion.43, bf16[480,5,128]{0,2,1:T(8,128)(2,1)S(1)} %bitcast.100, bf16[7680,5,128]{2,1,0:T(8,128)(2,1)} %reshape.104), kind=kOutput, calls=%fused_computation.2 | convolution fusion | flops 4773885440 | bytes 84190080 | tf_op jit(solution)/shard_map/qhd,khd->hqk/dot_general | solution.py:58
  349.6 3.8 fusion.10
  353.4 23.2 %fusion.1 = f32[5,480]{1,0:T(8,128)S(1)} fusion(f32[5,480,7680]{2,1,0:T(8,128)} %get-tuple-element.15, f32[5,480]{1,0:T(8,128)S(1)} %get-tuple-element.10, pred[7680]{0:T(1024)(128)(4,1)S(1)} %fusion.43), kind=kLoop, calls=%fused_computation.3 | loop fusion | flops 73725600 | bytes 73754880 | tf_op jit(solution)/shard_map/reduce_sum | solution.py:65
  376.7 1.7 fusion.30
  378.4 13.7 %copy.79 = bf16[1,7680,640]{1,2,0:T(8,128)(2,1)} copy(bf16[1,7680,640]{2,1,0:T(8,128)(2,1)} %all-gather.3.cloned.1.call-done) | data formatting | bytes 19660800 | tf_op jit(solution)/shard_map/all_gather | solution.py:91
  392.1 29.3 %fusion.36 = bf16[480,5,128]{2,0,1:T(8,128)(2,1)S(1)} fusion(f32[480,5,128]{2,0,1:T(8,128)S(1)} %fusion.30, bf16[7680,5,128]{0,2,1:T(8,128)(2,1)} %bitcast.98, f32[5,480,7680]{2,1,0:T(8,128)} %get-tuple-element.15, f32[5,480]{1,0:T(8,128)S(1)} %get-tuple-element.10, pred[7680]{0:T(1024)(128)(4,1)S(1)} %fusion.43, f32[480,5]{0,1:T(8,128)S(1)} %get-tuple-element.7), kind=kOutput, calls=%fused_computation.27 | convolution fusion | flops 4793241600 | bytes 85428480 | tf_op jit(solution)/shard_map/hqk,khd->hqd/dot_general | solution.py:66
  421.7 8.8 %fusion.8 = bf16[5120,480]{0,1:T(8,128)(2,1)} fusion(bf16[480,640]{0,1:T(8,128)(2,1)S(1)} %bitcast.114, bf16[640,5120]{1,0:T(8,128)(2,1)} %param.15), kind=kOutput, calls=%fused_computation.10 | convolution fusion | flops 3148185600 | bytes 12083200 | tf_op jit(solution)/shard_map/dot_general | solution.py:103
  430.5 7.8 %copy.94 = bf16[5120,480]{1,0:T(8,128)(2,1)} copy(bf16[5120,480]{0,1:T(8,128)(2,1)} %fusion.8) | data formatting | bytes 9830400
  438.4 65.0 %reduce-scatter.4.cloned.1.call-done = bf16[640,480]{1,0:T(8,128)(2,1)} async-done(((bf16[5120,480]{1,0:T(8,128)(2,1)}), bf16[640,480]{1,0:T(8,128)(2,1)}) %reduce-scatter.4.cloned.1.call-update) | async-done | bytes 614416
  503.4 1.4 copy.95
  504.8 1.9 copy.82
  507.3 4.9 reduce.13
  512.2 2.2 reshape.112
  514.4 3.7 all-to-all-start.2
  518.1 9.5 %all-to-all-done.2 = bf16[2,2,76800]{2,1,0:T(2,128)(2,1)S(1)} async-done(((bf16[2,2,76800]{2,1,0:T(2,128)(2,1)}), bf16[2,2,76800]{2,1,0:T(2,128)(2,1)S(1)}, u32[]{:S(2)}, u32[]{:S(2)}) %all-to-all-start.2) | async-done | bytes 614432 | tf_op jit(solution)/shard_map/all_to_all | solution.py:114
  527.6 1.3 reshape.113
  530.8 8.9 %all-to-all-start.3 = ((f32[16,1,1280]{2,1,0:T(1,128)}), f32[16,1,1280]{2,1,0:T(1,128)S(1)}, u32[]{:S(2)}, u32[]{:S(2)}) async-start(f32[16,1,1280]{2,1,0:T(1,128)} %broadcast_in_dim.102), calls=%async_computation.3 | async-start | bytes 163840 | tf_op jit(solution)/shard_map/all_to_all | solution.py:22
  540.3 7.5 %all-to-all-done.3 = f32[16,1,1280]{2,1,0:T(1,128)S(1)} async-done(((f32[16,1,1280]{2,1,0:T(1,128)}), f32[16,1,1280]{2,1,0:T(1,128)S(1)}, u32[]{:S(2)}, u32[]{:S(2)}) %all-to-all-start.3) | async-done | bytes 81952 | tf_op jit(solution)/shard_map/all_to_all | solution.py:22
  (41 shorter events, 6.6 us)
Async XLA Ops:
  29.6 6.1 %copy-start.2 = (bf16[1,480,640]{2,1,0:T(8,128)(2,1)S(1)}, bf16[1,480,640]{2,1,0:T(8,128)(2,1)}, u32[]{:S(2)}) copy-start(bf16[1,480,640]{2,1,0:T(8,128)(2,1)} %param.8) | copy-start | bytes 1843204
  29.6 7.0 %copy-start = (bf16[1,512,640]{2,1,0:T(8,128)(2,1)S(1)}, bf16[1,512,640]{2,1,0:T(8,128)(2,1)}, u32[]{:S(2)}) copy-start(bf16[1,512,640]{2,1,0:T(8,128)(2,1)} %param.11) | copy-start | bytes 1966084
  29.6 7.3 %copy-start.1 = (bf16[1,512,640]{2,1,0:T(8,128)(2,1)S(1)}, bf16[1,512,640]{2,1,0:T(8,128)(2,1)}, u32[]{:S(2)}) copy-start(bf16[1,512,640]{2,1,0:T(8,128)(2,1)} %param.12) | copy-start | bytes 1966084
  29.6 265.7 %all-to-all-start.1 = ((bf16[16,480,640]{2,1,0:T(8,128)(2,1)}), bf16[16,480,640]{2,1,0:T(8,128)(2,1)}, u32[]{:S(2)}, u32[]{:S(2)}) async-start(bf16[16,480,640]{2,1,0:T(8,128)(2,1)} %stack.3), calls=%async_computation.1 | async-start | bytes 19660800 | tf_op jit(solution)/shard_map/all_to_all | solution.py:89
  34.9 343.4 %all-gather.3.cloned.1.call-start = ((), (), s32[]{:S(2)}) async-start(), calls=%async_computation.5 | async-start | bytes 10444800 | tf_op jit(solution)/shard_map/all_gather | solution.py:91
  35.7 467.7 %reduce-scatter.4.cloned.1.call-start = ((), (), s32[]{:S(2)}) async-start(), calls=%async_computation.6 | async-start | bytes 5898240
  349.6 27.1 %slice-start = ((s8[4915200]{0:T(1024)(128)(4,1)}), s8[4194304]{0:T(1024)(128)(4,1)S(1)}, s32[]{:S(2)}) async-start(s8[4915200]{0:T(1024)(128)(4,1)} %bitcast.96), calls=%async_computation.7 | async-start | bytes 8388608
  353.4 23.3 %slice-start.1 = ((s8[4915200]{0:T(1024)(128)(4,1)}), s8[720896]{0:T(1024)(128)(4,1)S(1)}, s32[]{:S(2)}) async-start(s8[4915200]{0:T(1024)(128)(4,1)} %bitcast.96), calls=%async_computation.8 | async-start | bytes 1441792
  514.4 13.2 %all-to-all-start.2 = ((bf16[2,2,76800]{2,1,0:T(2,128)(2,1)}), bf16[2,2,76800]{2,1,0:T(2,128)(2,1)S(1)}, u32[]{:S(2)}, u32[]{:S(2)}) async-start(bf16[2,2,76800]{2,1,0:T(2,128)(2,1)} %reshape.112), calls=%async_computation.2 | async-start | bytes 1228800 | tf_op jit(solution)/shard_map/all_to_all | solution.py:114
  530.8 17.0 %all-to-all-start.3 = ((f32[16,1,1280]{2,1,0:T(1,128)}), f32[16,1,1280]{2,1,0:T(1,128)S(1)}, u32[]{:S(2)}, u32[]{:S(2)}) async-start(f32[16,1,1280]{2,1,0:T(1,128)} %broadcast_in_dim.102), calls=%async_computation.3 | async-start | bytes 163840 | tf_op jit(solution)/shard_map/all_to_all | solution.py:22
Sparse Core Ops, SparseCore 0:
  37.6 196.1 all-gather.2
  438.5 64.8 reduce-scatter.3
